TPU v7x, 32 devices: a whole 2x2x4 slice. The times are simulated.
32 devices in a mesh: kpt: 2 (over x), col: 4 (over z), row: 4 (over y, core).
Axes of the slice: x: 2, y: 2, z: 4, core: 2. Of those that a mesh axis runs over, the one named last changes fastest.
Arguments:
- h_slab: bfloat16 [8, 4, 2560, 5120], P(('kpt', 'row'), 'col'), parts along dimension 0
- h_diag: bfloat16 [8, 5120, 5120], P(('kpt', 'row'), 'col'), parts along dimension 0
- vec_occ: float32 [40960, 64], P(('kpt', 'row', 'col')), parts along dimension 0
- vec_virt: float32 [40960, 64], P(('kpt', 'row', 'col')), parts along dimension 0
Outputs:
- output 1: float32 [40960, 64], P(('kpt', 'row', 'col')), parts along dimension 0
- output 2: float32 [40960, 64], P(('kpt', 'row', 'col')), parts along dimension 0
There are 2 independent parts. A program takes and returns all parts, laid end to end along the dimension named above; each array names one.
All inputs are finite; a program needn't handle non-finite values.
Results may differ from a plain program's by a relative error of at most 0.001.
Values are sent between devices in bfloat16 or wider.
A program may use at most 1 GiB of HBM per device.

v0:
```python
import jax
import jax.numpy as jnp
from jax import lax
from jax.sharding import PartitionSpec as P

FILTER_STEPS = 3
CEN_OCC = 0.5
HW_OCC = 1.5
CEN_VIRT = -0.5
HW_VIRT = 1.5


def column_coeffs(half_vecs):
    col_shift = jnp.concatenate([jnp.full((half_vecs,), CEN_OCC, jnp.float32), jnp.full((half_vecs,), CEN_VIRT, jnp.float32)])
    col_scale = jnp.concatenate([jnp.full((half_vecs,), 1.0 / HW_OCC, jnp.float32), jnp.full((half_vecs,), 1.0 / HW_VIRT, jnp.float32)])
    return col_shift, col_scale


def solution(mesh):
    slab_spec = P(("kpt", "row"), "col", None, None)
    diag_spec = P(("kpt", "row"), "col", None)
    vec_spec = P(("kpt", "row", "col"), None)

    def local_filter(h_slab, h_diag, vec_occ, vec_virt):
        own_slab = h_slab[0, 0]
        diag_rows = h_diag[0]
        half_rows = own_slab.shape[0]
        half_vecs = vec_occ.shape[1]
        row_id = lax.axis_index("row")
        col_id = lax.axis_index("col")
        is_lower = row_id > col_id
        is_upper = row_id < col_id
        is_diag = row_id == col_id
        col_shift, col_scale = column_coeffs(half_vecs)

        def apply_op(cur_vecs):
            wire_vecs = cur_vecs.astype(jnp.bfloat16)
            row_panel = lax.all_gather(wire_vecs, "col", axis=0, tiled=True)
            col_panel = lax.psum(jnp.where(is_diag, row_panel, jnp.zeros_like(row_panel)), "row")
            left_panel = jnp.where(is_lower, col_panel, row_panel)
            right_half = jnp.where(is_lower, row_panel[:half_rows], col_panel[half_rows:])
            slab_prod = jnp.dot(own_slab, left_panel, preferred_element_type=jnp.float32)
            tran_prod = lax.dot_general(own_slab, right_half, (((0,), (0,)), ((), ())), preferred_element_type=jnp.float32)
            zero_half = jnp.zeros_like(slab_prod)
            to_row = jnp.where(is_lower, jnp.concatenate([slab_prod, zero_half], axis=0), jnp.where(is_upper, tran_prod, 0.0))
            to_col = jnp.where(is_lower, tran_prod, jnp.where(is_upper, jnp.concatenate([zero_half, slab_prod], axis=0), 0.0))
            col_full = lax.psum(to_col, "row")
            row_total = to_row + jnp.where(is_diag, col_full, 0.0)
            row_sum = lax.psum_scatter(row_total, "col", scatter_dimension=0, tiled=True)
            diag_prod = jnp.dot(diag_rows, row_panel, preferred_element_type=jnp.float32)
            return row_sum + diag_prod

        prev_vecs = jnp.concatenate([vec_occ, vec_virt], axis=1)
        cur_vecs = (apply_op(prev_vecs) - col_shift * prev_vecs) * col_scale
        for _ in range(FILTER_STEPS - 1):
            next_vecs = 2.0 * ((apply_op(cur_vecs) - col_shift * cur_vecs) * col_scale) - prev_vecs
            prev_vecs, cur_vecs = cur_vecs, next_vecs
        return cur_vecs[:, :half_vecs], cur_vecs[:, half_vecs:]

    return jax.shard_map(local_filter, mesh=mesh, in_specs=(slab_spec, diag_spec, vec_spec, vec_spec), out_specs=(vec_spec, vec_spec), check_vma=False)
```

profile of v0, /device:TPU:0, one launch (start us, length us, event | category | flops | bytes accessed | tf_op | source)
XLA Modules:
  0.0 702.9 jit_solution(1362346496169282055)
XLA Ops:
  10.1 35.0 %all-gather.4.cloned.1.call-done = bf16[5120,128]{0,1:T(8,128)(2,1)} async-done(((bf16[1280,128]{0,1:T(8,128)(2,1)}), bf16[5120,128]{0,1:T(8,128)(2,1)}) %all-gather.4.cloned.1.call-update) | async-done | bytes 1310736 | tf_op jit(solution)/shard_map/all_gather | solution.py:38
  47.7 38.6 %all-reduce.13.cloned.1.call-done = bf16[5120,128]{0,1:T(8,128)(2,1)} async-done(((bf16[5120,128]{0,1:T(8,128)(2,1)}), bf16[5120,128]{0,1:T(8,128)(2,1)}) %all-reduce.13.cloned.1.call-update) | async-done | bytes 1310736 | tf_op jit(solution)/shard_map/psum | solution.py:39
  86.3 13.6 %fusion.27 = f32[2560,128]{0,1:T(8,128)S(1)} fusion(bf16[1,1,2560,5120]{3,2,1,0:T(8,128)(2,1)} %param.4, bf16[5120,128]{0,1:T(8,128)(2,1)} %all-reduce.13.cloned.1.call-done, bf16[5120,128]{0,1:T(8,128)(2,1)S(1)} %copy-done, pred[]{:T(512)S(6)} %gt.3), kind=kOutput, calls=%fused_computation.21 | convolution fusion | flops 3356098560 | bytes 30146560 | tf_op jit(solution)/shard_map/dot_general | solution.py:42
  99.9 14.6 %select_select_fusion.2 = (f32[5120,128]{0,1:T(8,128)}, f32[5120,128]{0,1:T(8,128)}) fusion(f32[2560,128]{0,1:T(8,128)S(1)} %fusion.27, pred[]{:T(512)S(6)} %lt.3, pred[]{:T(512)S(6)} %gt.3, bf16[1,1,2560,5120]{3,2,1,0:T(8,128)(2,1)} %param.4, bf16[5120,128]{0,1:T(8,128)(2,1)} %all-reduce.13.cloned.1.call-done, bf16[5120,128]{0,1:T(8,128)(2,1)S(1)} %copy-done), kind=kOutput, calls=%fused_computation.29 | convolution fusion | flops 3357081600 | bytes 34080256 | tf_op jit(solution)/shard_map/dot_general | solution.py:43
  114.6 59.8 %all-reduce.15.cloned.1.call-done = f32[5120,128]{0,1:T(8,128)} async-done(((f32[5120,128]{0,1:T(8,128)}), f32[5120,128]{0,1:T(8,128)}) %all-reduce.15.cloned.1.call-update) | async-done | bytes 2621456 | tf_op jit(solution)/shard_map/psum | solution.py:47
  174.5 3.7 select_add_fusion.2
  178.2 52.5 %reduce-scatter.4.cloned.1.call-done = f32[1280,128]{0,1:T(8,128)} async-done(((f32[5120,128]{0,1:T(8,128)}), f32[1280,128]{0,1:T(8,128)}) %reduce-scatter.4.cloned.1.call-update) | async-done | bytes 655376 | tf_op jit(solution)/shard_map/reduce_scatter | solution.py:49
  230.7 10.1 %multiply_convert_fusion = (bf16[1280,128]{0,1:T(8,128)(2,1)}, f32[1280,128]{0,1:T(8,128)}) fusion(f32[1280,128]{0,1:T(8,128)S(1)} %constant_dynamic-update-slice_fusion, f32[128]{0:T(128)S(1)} %copy-done.6, f32[1280,128]{0,1:T(8,128)} %reduce-scatter.4.cloned.1.call-done, bf16[5120,128]{0,1:T(8,128)(2,1)S(1)} %copy-done, bf16[1,1280,5120]{2,1,0:T(8,128)(2,1)} %param.5), kind=kOutput, calls=%fused_computation.61 | convolution fusion | flops 1678540800 | bytes 16712192 | tf_op jit(solution)/shard_map/dot_general | solution.py:50
  240.9 31.7 %all-gather.6.cloned.1.call-done = bf16[5120,128]{0,1:T(8,128)(2,1)} async-done(((bf16[1280,128]{0,1:T(8,128)(2,1)}), bf16[5120,128]{0,1:T(8,128)(2,1)}) %all-gather.6.cloned.1.call-update) | async-done | bytes 1310736 | tf_op jit(solution)/shard_map/all_gather | solution.py:38
  275.4 38.4 %all-reduce.17.cloned.1.call-done = bf16[5120,128]{0,1:T(8,128)(2,1)} async-done(((bf16[5120,128]{0,1:T(8,128)(2,1)}), bf16[5120,128]{0,1:T(8,128)(2,1)}) %all-reduce.17.cloned.1.call-update) | async-done | bytes 1310736 | tf_op jit(solution)/shard_map/psum | solution.py:39
  313.9 13.6 %fusion.30 = f32[2560,128]{0,1:T(8,128)S(1)} fusion(bf16[1,1,2560,5120]{3,2,1,0:T(8,128)(2,1)} %param.4, bf16[5120,128]{0,1:T(8,128)(2,1)} %all-reduce.17.cloned.1.call-done, bf16[5120,128]{0,1:T(8,128)(2,1)S(1)} %copy-done.1, pred[]{:T(512)S(6)} %gt.3), kind=kOutput, calls=%fused_computation.22 | convolution fusion | flops 3356098560 | bytes 30146560 | tf_op jit(solution)/shard_map/dot_general | solution.py:42
  327.5 14.6 %select_select_fusion.1 = (f32[5120,128]{0,1:T(8,128)}, f32[5120,128]{0,1:T(8,128)}) fusion(f32[2560,128]{0,1:T(8,128)S(1)} %fusion.30, pred[]{:T(512)S(6)} %lt.3, pred[]{:T(512)S(6)} %gt.3, bf16[1,1,2560,5120]{3,2,1,0:T(8,128)(2,1)} %param.4, bf16[5120,128]{0,1:T(8,128)(2,1)} %all-reduce.17.cloned.1.call-done, bf16[5120,128]{0,1:T(8,128)(2,1)S(1)} %copy-done.1), kind=kOutput, calls=%fused_computation.27 | convolution fusion | flops 3357081600 | bytes 34080256 | tf_op jit(solution)/shard_map/dot_general | solution.py:43
  342.2 59.8 %all-reduce.19.cloned.1.call-done = f32[5120,128]{0,1:T(8,128)} async-done(((f32[5120,128]{0,1:T(8,128)}), f32[5120,128]{0,1:T(8,128)}) %all-reduce.19.cloned.1.call-update) | async-done | bytes 2621456 | tf_op jit(solution)/shard_map/psum | solution.py:47
  402.0 3.7 select_add_fusion.1
  405.8 52.5 %reduce-scatter.6.cloned.1.call-done = f32[1280,128]{0,1:T(8,128)} async-done(((f32[5120,128]{0,1:T(8,128)}), f32[1280,128]{0,1:T(8,128)}) %reduce-scatter.6.cloned.1.call-update) | async-done | bytes 655376 | tf_op jit(solution)/shard_map/reduce_scatter | solution.py:49
  458.3 10.2 %fusion.88 = (bf16[1280,128]{0,1:T(8,128)(2,1)}, f32[1280,128]{0,1:T(8,128)}) fusion(f32[1280,128]{0,1:T(8,128)S(1)} %constant_dynamic-update-slice_fusion, f32[1280,128]{0,1:T(8,128)S(1)} %copy-done.3, f32[128]{0:T(128)S(1)} %copy-done.7, f32[1280,128]{0,1:T(8,128)} %reduce-scatter.6.cloned.1.call-done, bf16[5120,128]{0,1:T(8,128)(2,1)S(1)} %copy-done.1, ...), kind=kOutput, calls=%fused_computation.65 | convolution fusion | flops 1678704640 | bytes 17367552 | tf_op jit(solution)/shard_map/dot_general | solution.py:50
  468.5 31.7 %all-gather.8.cloned.1.call-done = bf16[5120,128]{0,1:T(8,128)(2,1)} async-done(((bf16[1280,128]{0,1:T(8,128)(2,1)}), bf16[5120,128]{0,1:T(8,128)(2,1)}) %all-gather.8.cloned.1.call-update) | async-done | bytes 1310736 | tf_op jit(solution)/shard_map/all_gather | solution.py:38
  503.1 38.4 %all-reduce.21.cloned.1.call-done = bf16[5120,128]{0,1:T(8,128)(2,1)} async-done(((bf16[5120,128]{0,1:T(8,128)(2,1)}), bf16[5120,128]{0,1:T(8,128)(2,1)}) %all-reduce.21.cloned.1.call-update) | async-done | bytes 1310736 | tf_op jit(solution)/shard_map/psum | solution.py:39
  541.5 13.6 %fusion.33 = f32[2560,128]{0,1:T(8,128)S(1)} fusion(bf16[1,1,2560,5120]{3,2,1,0:T(8,128)(2,1)} %param.4, bf16[5120,128]{0,1:T(8,128)(2,1)} %all-reduce.21.cloned.1.call-done, bf16[5120,128]{0,1:T(8,128)(2,1)S(1)} %copy-done.2, pred[]{:T(512)S(6)} %gt.3), kind=kOutput, calls=%fused_computation.23 | convolution fusion | flops 3356098560 | bytes 30146560 | tf_op jit(solution)/shard_map/dot_general | solution.py:42
  555.1 14.6 %select_select_fusion = (f32[5120,128]{0,1:T(8,128)}, f32[5120,128]{0,1:T(8,128)}) fusion(f32[2560,128]{0,1:T(8,128)S(1)} %fusion.33, pred[]{:T(512)S(6)} %lt.3, pred[]{:T(512)S(6)} %gt.3, bf16[1,1,2560,5120]{3,2,1,0:T(8,128)(2,1)} %param.4, bf16[5120,128]{0,1:T(8,128)(2,1)} %all-reduce.21.cloned.1.call-done, bf16[5120,128]{0,1:T(8,128)(2,1)S(1)} %copy-done.2), kind=kOutput, calls=%fused_computation.25 | convolution fusion | flops 3357081600 | bytes 34080256 | tf_op jit(solution)/shard_map/dot_general | solution.py:43
  569.8 59.8 %all-reduce.23.cloned.1.call-done = f32[5120,128]{0,1:T(8,128)} async-done(((f32[5120,128]{0,1:T(8,128)}), f32[5120,128]{0,1:T(8,128)}) %all-reduce.23.cloned.1.call-update) | async-done | bytes 2621456 | tf_op jit(solution)/shard_map/psum | solution.py:47
  629.6 3.7 select_add_fusion
  633.4 52.5 %reduce-scatter.8.cloned.1.call-done = f32[1280,128]{0,1:T(8,128)} async-done(((f32[5120,128]{0,1:T(8,128)}), f32[1280,128]{0,1:T(8,128)}) %reduce-scatter.8.cloned.1.call-update) | async-done | bytes 655376 | tf_op jit(solution)/shard_map/reduce_scatter | solution.py:49
  685.9 9.3 %fusion.72 = f32[1280,128]{0,1:T(8,128)S(1)} fusion(f32[1280,128]{0,1:T(8,128)} %reduce-scatter.8.cloned.1.call-done, bf16[5120,128]{0,1:T(8,128)(2,1)S(1)} %copy-done.2, bf16[1,1280,5120]{2,1,0:T(8,128)(2,1)} %param.5, f32[1280,128]{0,1:T(8,128)S(1)} %copy-done.5, f32[1280,128]{0,1:T(8,128)S(1)} %copy-done.4, f32[128]{0:T(128)S(1)} %copy-done.6), kind=kOutput, calls=%fused_computation.42 | convolution fusion | flops 1678704640 | bytes 17039872 | tf_op jit(solution)/shard_map/dot_general | solution.py:50
  (47 shorter events, 12.4 us)
Async XLA Ops:
  7.2 37.9 %all-gather.4.cloned.1.call-start = ((), (), s32[]{:S(2)}) async-start(), calls=%async_computation.3 | async-start | bytes 1638400 | tf_op jit(solution)/shard_map/all_gather | solution.py:38
  10.0 76.3 %all-reduce.13.cloned.1.call-start = ((), (), s32[]{:S(2)}) async-start(), calls=%async_computation.4 | async-start | bytes 2621440 | tf_op jit(solution)/shard_map/psum | solution.py:39
  45.1 41.2 %copy-start = (bf16[5120,128]{0,1:T(8,128)(2,1)S(1)}, bf16[5120,128]{0,1:T(8,128)(2,1)}, u32[]{:S(2)}) copy-start(bf16[5120,128]{0,1:T(8,128)(2,1)} %all-gather.4.cloned.1.call-done) | copy-start | bytes 3932164
  47.7 126.8 %all-reduce.15.cloned.1.call-start = ((), (), s32[]{:S(2)}) async-start(), calls=%async_computation.5 | async-start | bytes 5242880 | tf_op jit(solution)/shard_map/psum | solution.py:47
  114.6 116.1 %reduce-scatter.4.cloned.1.call-start = ((), (), s32[]{:S(2)}) async-start(), calls=%async_computation.6 | async-start | bytes 3276800 | tf_op jit(solution)/shard_map/reduce_scatter | solution.py:49
  178.2 52.5 %copy-start.6 = (f32[128]{0:T(128)S(1)}, f32[128]{0:T(128)}, u32[]{:S(2)}) copy-start(f32[128]{0:T(128)} %constant.19.clone.1) | copy-start | bytes 1540
  178.2 94.4 %all-gather.6.cloned.1.call-start = ((), (), s32[]{:S(2)}) async-start(), calls=%async_computation.7 | async-start | bytes 1638400 | tf_op jit(solution)/shard_map/all_gather | solution.py:38
  240.9 73.0 %all-reduce.17.cloned.1.call-start = ((), (), s32[]{:S(2)}) async-start(), calls=%async_computation.8 | async-start | bytes 2621440 | tf_op jit(solution)/shard_map/psum | solution.py:39
  272.6 41.2 %copy-start.1 = (bf16[5120,128]{0,1:T(8,128)(2,1)S(1)}, bf16[5120,128]{0,1:T(8,128)(2,1)}, u32[]{:S(2)}) copy-start(bf16[5120,128]{0,1:T(8,128)(2,1)} %all-gather.6.cloned.1.call-done) | copy-start | bytes 3932164
  275.2 126.8 %all-reduce.19.cloned.1.call-start = ((), (), s32[]{:S(2)}) async-start(), calls=%async_computation.9 | async-start | bytes 5242880 | tf_op jit(solution)/shard_map/psum | solution.py:47
  342.1 116.1 %reduce-scatter.6.cloned.1.call-start = ((), (), s32[]{:S(2)}) async-start(), calls=%async_computation.10 | async-start | bytes 3276800 | tf_op jit(solution)/shard_map/reduce_scatter | solution.py:49
  405.7 52.5 %copy-start.3 = (f32[1280,128]{0,1:T(8,128)S(1)}, f32[1280,128]{0,1:T(8,128)}, u32[]{:S(2)}) copy-start(f32[1280,128]{0,1:T(8,128)} %get-tuple-element.7) | copy-start | bytes 1966084
  405.7 52.5 %copy-start.7 = (f32[128]{0:T(128)S(1)}, f32[128]{0:T(128)}, u32[]{:S(2)}) copy-start(f32[128]{0:T(128)} %constant.21.clone.1) | copy-start | bytes 1540
  405.8 94.5 %all-gather.8.cloned.1.call-start = ((), (), s32[]{:S(2)}) async-start(), calls=%async_computation.11 | async-start | bytes 1638400 | tf_op jit(solution)/shard_map/all_gather | solution.py:38
  468.5 73.0 %all-reduce.21.cloned.1.call-start = ((), (), s32[]{:S(2)}) async-start(), calls=%async_computation.12 | async-start | bytes 2621440 | tf_op jit(solution)/shard_map/psum | solution.py:39
  500.2 41.2 %copy-start.2 = (bf16[5120,128]{0,1:T(8,128)(2,1)S(1)}, bf16[5120,128]{0,1:T(8,128)(2,1)}, u32[]{:S(2)}) copy-start(bf16[5120,128]{0,1:T(8,128)(2,1)} %all-gather.8.cloned.1.call-done) | copy-start | bytes 3932164
  502.8 126.8 %all-reduce.23.cloned.1.call-start = ((), (), s32[]{:S(2)}) async-start(), calls=%async_computation.13 | async-start | bytes 5242880 | tf_op jit(solution)/shard_map/psum | solution.py:47
  569.7 116.1 %reduce-scatter.8.cloned.1.call-start = ((), (), s32[]{:S(2)}) async-start(), calls=%async_computation.14 | async-start | bytes 3276800 | tf_op jit(solution)/shard_map/reduce_scatter | solution.py:49
  633.3 52.5 %copy-start.4 = (f32[1280,128]{0,1:T(8,128)S(1)}, f32[1280,128]{0,1:T(8,128)}, u32[]{:S(2)}) copy-start(f32[1280,128]{0,1:T(8,128)} %get-tuple-element.7) | copy-start | bytes 1966084
  633.3 52.5 %copy-start.5 = (f32[1280,128]{0,1:T(8,128)S(1)}, f32[1280,128]{0,1:T(8,128)}, u32[]{:S(2)}) copy-start(f32[1280,128]{0,1:T(8,128)} %get-tuple-element.11) | copy-start | bytes 1966084
Sparse Core Ops, SparseCore 0:
  10.1 34.9 all-gather.3
  47.8 38.4 all-reduce.12
  114.7 59.7 all-reduce.14
  178.3 52.3 reduce-scatter.3
  241.0 31.5 all-gather.5
  275.3 38.4 all-reduce.16
  342.3 59.7 all-reduce.18
  405.9 52.3 reduce-scatter.5
  468.6 31.5 all-gather.7
  502.9 38.4 all-reduce.20
  569.9 59.7 all-reduce.22
  633.5 52.3 reduce-scatter.7
where the time goes:
time: 703 us
  waiting for transfers between devices  551 us (78%)
  matrix products  114 us (16%)
  other arithmetic  19.5 us (3%)
  between operations  14.3 us (2%)
    psum x3, waiting for transfers between devices, apply_op(): col_full = lax.psum(to_col, 'row')  180 us
    reduce_scatter x3, waiting for transfers between devices, apply_op(): lax.psum_scatter(row_total, 'col', scatter_dimension=0, tiled=True)  157 us
    psum x3, waiting for transfers between devices, apply_op(): lax.psum(jnp.where(is_diag, row_panel, jnp.zeros_like(row_panel)), 'row')  115 us
    all_gather x3, waiting for transfers between devices, apply_op(): row_panel = lax.all_gather(wire_vecs, 'col', axis=0, tiled=True)  98.4 us
    dot_general x3, matrix products, apply_op(): lax.dot_general(own_slab, right_half, (((0,), (0,)), ((), ())), preferred...  43.9 us
    dot_general x3, matrix products, apply_op(): jnp.dot(own_slab, left_panel, preferred_element_type=jnp.float32)  40.8 us
    dot_general x3, matrix products, apply_op(): jnp.dot(diag_rows, row_panel, preferred_element_type=jnp.float32)  29.6 us
  transfers between devices with their start and end apart: 12, of which 12 were waited for; matrix products, arithmetic and copies ran while one was open for 0% of the time, Pallas kernels for 0%

commit v1 on v0

v1 whole, which is shorter than its diff:
```python
import jax
import jax.numpy as jnp
from jax import lax
from jax.experimental import pallas as pl
from jax.experimental.pallas import tpu as pltpu
from jax.sharding import PartitionSpec as P

FILTER_STEPS = 3
CEN_OCC = 0.5
CEN_VIRT = -0.5
HALF_WIDTH = 1.5
SIDE = 4
HALVES = 2
UNITS = FILTER_STEPS * HALVES
DIAG_ACC = 8
MESH = pl.DeviceIdType.MESH
NN = (((1,), (0,)), ((), ()))
NT = (((1,), (1,)), ((), ()))


def filter_kernel(slab_hbm, strip_hbm, occ_ref, virt_ref, out_occ, out_virt,
                  mat, vec, acc, red, col, cur, prev,
                  mat_sem, vec_send, vec_recv, colvec_recv, acc_send, red_recv, col_recv):
    seg_rows = cur.shape[-1]
    kpt = lax.axis_index("kpt")
    c = lax.axis_index("col")
    r = lax.axis_index("row")
    is_diag = r == c
    lower = r > c
    upper = r < c
    chip = r // 2
    core = r % 2
    partner = r + 1 - 2 * core
    same_chip = (c // 2) == chip
    far0 = 2 * (1 - chip)
    col_peers = (partner, far0, far0 + 1)
    diag_dev = (kpt, c, c)

    def seg_order(i):
        ahead = jnp.where(c == 1, jnp.where(i < 2, 3 - i, i - 2), jnp.where(i < 2, i, 5 - i))
        return jnp.where(c == 0, 3 - i, jnp.where(c == 3, i, ahead))

    def goes_right(cc, seg):
        return (seg < 2) | (r <= cc)

    def goes_left(cc, seg):
        return ~((r == 3) & (cc == 3) & (seg < 2))

    def sends(seg):
        return jnp.where(seg > c, goes_right(c, seg), goes_left(c, seg)) & (seg != c)

    def from_left(seg):
        return (c > 0) & goes_right(c - 1, seg)

    def from_right(seg):
        return (c < 3) & goes_left(c + 1, seg)

    def incoming(seg):
        return jnp.where(seg > c, from_left(seg), from_right(seg))

    def row_copy(h, b, seg, way):
        return pltpu.make_async_remote_copy(
            src_ref=vec.at[h, b, 0, seg], dst_ref=vec.at[h, b, 0, seg],
            send_sem=vec_send.at[h, way, seg], recv_sem=vec_recv.at[h, b, seg],
            device_id=(kpt, c + 1 - 2 * way, r), device_id_type=MESH)

    def col_copy(h, b, seg, peer):
        return pltpu.make_async_remote_copy(
            src_ref=vec.at[h, b, 0, seg], dst_ref=vec.at[h, b, 1, seg],
            send_sem=vec_send.at[h, 2 + peer, seg], recv_sem=colvec_recv.at[h, b, seg],
            device_id=(kpt, c, col_peers[peer]), device_id_type=MESH)

    def red_copy(h, seg):
        step = jnp.where(seg > c, 1, -1)
        slot = jnp.where(seg == c - 1, SIDE, seg)
        return pltpu.make_async_remote_copy(
            src_ref=acc.at[h, seg], dst_ref=red.at[h, slot],
            send_sem=acc_send.at[h, seg], recv_sem=red_recv.at[h, slot],
            device_id=(kpt, c + step, r), device_id_type=MESH)

    def sum_copy(h, seg, slot, dev):
        return pltpu.make_async_remote_copy(
            src_ref=acc.at[h, SIDE + seg], dst_ref=col.at[h, slot, seg],
            send_sem=acc_send.at[h, SIDE + seg], recv_sem=col_recv.at[h, slot, seg],
            device_id=dev, device_id_type=MESH)

    def send_row(h, b, seg, left_ok, right_ok):
        @pl.when((c < 3) & right_ok)
        def _():
            row_copy(h, b, seg, 0).start()

        @pl.when((c > 0) & left_ok)
        def _():
            row_copy(h, b, seg, 1).start()

    def send_col(h, b, seg):
        for peer in range(3):
            @pl.when(is_diag & ((col_peers[peer] > c) | (seg >= 2)))
            def _():
                col_copy(h, b, seg, peer).start()

    def wait_vec_sends(h, b):
        def each(seg, carry):
            @pl.when((c < 3) & (seg <= c))
            def _():
                row_copy(h, b, seg, 0).wait_send()

            @pl.when((c > 0) & (seg >= c))
            def _():
                row_copy(h, b, seg, 1).wait_send()

            for peer in range(3):
                @pl.when(is_diag & ((col_peers[peer] > c) | (seg >= 2)))
                def _():
                    col_copy(h, b, seg, peer).wait_send()
            return carry

        lax.fori_loop(0, SIDE, each, 0)

    def wait_acc_sends(h):
        def each(seg, carry):
            @pl.when(sends(seg))
            def _():
                red_copy(h, seg).wait_send()

            @pl.when(~is_diag & (lower | (seg >= 2)))
            def _():
                sum_copy(h, seg, 0, diag_dev).wait_send()
            return carry

        lax.fori_loop(0, SIDE, each, 0)

    def wait_colvec(h, b, seg):
        col_copy(h, b, seg, 0).wait_recv()

    def send_sum(h, seg):
        @pl.when(same_chip)
        def _():
            sum_copy(h, seg, 0, diag_dev).start()

        @pl.when(~same_chip & (seg % 2 != core))
        def _():
            sum_copy(h, seg, 0, (kpt, c, partner)).start()

    def combine_sums(h):
        first = jnp.where(lower, 0, 1)

        def each(i, carry):
            seg = 2 * i + core
            sum_copy(h, seg, 0, diag_dev).wait_recv()
            acc[h, SIDE + seg] += col[h, 0, seg]
            sum_copy(h, seg, 1, diag_dev).start()
            return carry

        @pl.when(~same_chip)
        def _():
            lax.fori_loop(first, 2, each, 0)

    def column_total(h):
        def each(i, carry):
            seg = seg_order(i)
            near = (partner > c) | (seg >= 2)
            far = (far0 > c) | (seg >= 2)

            @pl.when(near)
            def _():
                sum_copy(h, seg, 0, diag_dev).wait_recv()
                acc[h, seg] += col[h, 0, seg]

            @pl.when(far)
            def _():
                sum_copy(h, seg, 1, diag_dev).wait_recv()
                acc[h, seg] += col[h, 1, seg]

            @pl.when(sends(seg) & ~incoming(seg))
            def _():
                red_copy(h, seg).start()
            return carry

        lax.fori_loop(0, SIDE, each, 0)

    def relay(h, seg):
        @pl.when(sends(seg) & incoming(seg))
        def _():
            pltpu.make_async_remote_copy(
                src_ref=acc.at[h, seg], dst_ref=red.at[h, seg],
                send_sem=acc_send.at[h, seg], recv_sem=red_recv.at[h, seg],
                device_id=diag_dev, device_id_type=MESH).wait_recv()
            acc[h, seg] += red[h, seg]
            red_copy(h, seg).start()

    def take_piece(k, h, b, seg):
        n_nt = jnp.where(upper, 3, 1)
        n_nn = jnp.where(lower & (seg < 2), SIDE, 0)

        def nt_step(i, carry):
            block = jnp.where(i == 0, 2 * SIDE + seg, (i - 1) * SIDE + seg)
            dest = jnp.where(i == 0, DIAG_ACC, SIDE + 1 + i)

            @pl.when(k == 0)
            def _():
                pltpu.make_async_copy(mat.at[block], mat.at[block], mat_sem.at[block]).wait()
            acc[h, dest] += lax.dot_general(vec[h, b, 0, seg], mat[block], NT, preferred_element_type=jnp.float32)
            return carry

        lax.fori_loop(0, n_nt, nt_step, 0)

        def nn_step(i, carry):
            block = seg * SIDE + i

            @pl.when(k == 0)
            def _():
                pltpu.make_async_copy(mat.at[block], mat.at[block], mat_sem.at[block]).wait()
            acc[h, SIDE + i] += lax.dot_general(vec[h, b, 0, seg], mat[block], NN, preferred_element_type=jnp.float32)
            return carry

        lax.fori_loop(0, n_nn, nn_step, 0)

    def upper_row_terms(h, b):
        def each(i, carry):
            seg = seg_order(i // 2)
            half = i % 2
            acc[h, seg] += lax.dot_general(
                vec[h, b, 1, 2 + half], mat[half * SIDE + seg], NN, preferred_element_type=jnp.float32)
            return carry

        lax.fori_loop(0, 2 * SIDE, each, 0)

    def lower_row_terms(h, b):
        def each(i, carry):
            seg = (i // 2 + c) % SIDE
            half = i % 2

            @pl.when((half == 0) & (i > 0))
            def _():
                wait_colvec(h, b, seg)
            acc[h, half] += lax.dot_general(
                vec[h, b, 1, seg], mat[half * SIDE + seg], NT, preferred_element_type=jnp.float32)
            return carry

        lax.fori_loop(0, 2 * SIDE, each, 0)

    def finish(k, h, b, next_b):
        wait_vec_sends(h, b)

        @pl.when(from_left(c))
        def _():
            pltpu.make_async_remote_copy(
                src_ref=acc.at[h, c], dst_ref=red.at[h, c],
                send_sem=acc_send.at[h, c], recv_sem=red_recv.at[h, c],
                device_id=diag_dev, device_id_type=MESH).wait_recv()
            acc[h, c] += red[h, c]

        @pl.when(from_right(c))
        def _():
            pltpu.make_async_remote_copy(
                src_ref=acc.at[h, c], dst_ref=red.at[h, SIDE],
                send_sem=acc_send.at[h, c], recv_sem=red_recv.at[h, SIDE],
                device_id=diag_dev, device_id_type=MESH).wait_recv()
            acc[h, c] += red[h, SIDE]

        center = jnp.where(h == 0, CEN_OCC, CEN_VIRT)
        applied = acc[h, c] + acc[h, DIAG_ACC]
        scaled = (applied - center * cur[h]) * (1.0 / HALF_WIDTH)
        first = k < HALVES
        nxt = jnp.where(first, scaled, 2.0 * scaled - prev[h])
        prev[h] = cur[h]
        cur[h] = nxt

        @pl.when(k + HALVES < UNITS)
        def _():
            vec[h, next_b, 0, c] = nxt.astype(jnp.bfloat16)
            send_row(h, next_b, c, True, True)
            send_col(h, next_b, c)

    barrier = pltpu.get_barrier_semaphore()

    @pl.when(c > 0)
    def _():
        pl.semaphore_signal(barrier, inc=1, device_id=(kpt, c - 1, r), device_id_type=MESH)

    @pl.when(c < 3)
    def _():
        pl.semaphore_signal(barrier, inc=1, device_id=(kpt, c + 1, r), device_id_type=MESH)

    for peer in range(3):
        pl.semaphore_signal(barrier, inc=1, device_id=(kpt, c, col_peers[peer]), device_id_type=MESH)

    def load_block(i, carry):
        seg = (c + i) % SIDE
        pltpu.make_async_copy(
            strip_hbm.at[:, pl.ds(pl.multiple_of(seg * seg_rows, seg_rows), seg_rows)],
            mat.at[2 * SIDE + seg], mat_sem.at[2 * SIDE + seg]).start()

        @pl.when(~is_diag)
        def _():
            for half in range(2):
                pltpu.make_async_copy(
                    slab_hbm.at[pl.ds(half * seg_rows, seg_rows),
                                pl.ds(pl.multiple_of(seg * seg_rows, seg_rows), seg_rows)],
                    mat.at[half * SIDE + seg], mat_sem.at[half * SIDE + seg]).start()
        return carry

    lax.fori_loop(0, SIDE, load_block, 0)
    for h, src in enumerate((occ_ref, virt_ref)):
        cur[h] = src[...]
        prev[h] = jnp.zeros_like(src)
        vec[h, 0, 0, c] = src[...].astype(jnp.bfloat16)
    pl.semaphore_wait(barrier, 3 + (c > 0).astype(jnp.int32) + (c < 3).astype(jnp.int32))
    for h in range(HALVES):
        send_row(h, 0, c, True, True)
        send_col(h, 0, c)

    def slot(k, carry):
        h = k % 2
        b = (k // 2) % 2
        last = k - 1
        lh = (k + 1) % 2
        lb = ((k + 1) // 2 + 1) % 2
        live = k < UNITS
        older = k >= 1

        @pl.when(live)
        def _():
            @pl.when(k >= HALVES)
            def _():
                wait_acc_sends(h)

            def clear(i, cc):
                acc[h, i] = jnp.zeros(acc.shape[2:], acc.dtype)
                return cc

            lax.fori_loop(0, DIAG_ACC + 1, clear, 0)

        def arrivals(d, cc):
            def side(s, ccc):
                seg = c + (2 * s - 1) * d
                valid = live & (seg >= 0) & (seg < SIDE) & ((d > 0) | (s == 0))

                @pl.when(valid)
                def _():
                    @pl.when(d > 0)
                    def _():
                        row_copy(h, b, seg, 0).wait_recv()
                        send_row(h, b, seg, s == 1, s == 0)
                        send_col(h, b, seg)
                    take_piece(k, h, b, seg)
                return ccc

            lax.fori_loop(0, 2, side, 0)

            @pl.when(live & lower & (d == jnp.where(c == 2, 2, 1)))
            def _():
                wait_colvec(h, b, c)

                def each(i, ccc):
                    send_sum(h, seg_order(i))
                    return ccc

                lax.fori_loop(0, SIDE, each, 0)

            @pl.when(live & lower & (d == 2))
            def _():
                combine_sums(h)

            @pl.when(older & is_diag & (c >= 2) & (d == 1))
            def _():
                column_total(lh)

            @pl.when(older & (c > 0) & (c < 3) & (d > 0))
            def _():
                relay(lh, jnp.where(c == 1, jnp.where(d == 3, 0, 4 - d), jnp.where(d == 3, 3, d - 1)))
            return cc

        lax.fori_loop(0, SIDE, arrivals, 0)

        @pl.when(live & upper)
        def _():
            wait_colvec(h, b, 2)
            wait_colvec(h, b, 3)
            send_sum(h, 2)
            send_sum(h, 3)
            upper_row_terms(h, b)
            combine_sums(h)

        @pl.when(live & lower)
        def _():
            lower_row_terms(h, b)

        @pl.when(older)
        def _():
            finish(last, lh, lb, 1 - lb)

        @pl.when(live & ~is_diag)
        def _():
            def each(i, cc):
                seg = seg_order(i)

                @pl.when(sends(seg) & ~incoming(seg))
                def _():
                    red_copy(h, seg).start()
                return cc

            lax.fori_loop(0, SIDE, each, 0)

        @pl.when(live & is_diag & (c < 2))
        def _():
            column_total(h)
        return carry

    lax.fori_loop(0, UNITS + 1, slot, 0)
    for h in range(HALVES):
        wait_acc_sends(h)
    out_occ[...] = cur[0]
    out_virt[...] = cur[1]


def solution(mesh):
    slab_spec = P(("kpt", "row"), "col", None, None)
    diag_spec = P(("kpt", "row"), "col", None)
    vec_spec = P(("kpt", "row", "col"), None)

    def local_filter(h_slab, h_diag, vec_occ, vec_virt):
        seg_rows, n_vecs = vec_occ.shape
        panel = (n_vecs, seg_rows)
        out = jax.ShapeDtypeStruct(panel, jnp.float32)
        vmem = pl.BlockSpec(memory_space=pltpu.VMEM)
        hbm = pl.BlockSpec(memory_space=pl.ANY)
        dma = pltpu.SemaphoreType.DMA
        filt_occ, filt_virt = pl.pallas_call(
            filter_kernel,
            out_shape=(out, out),
            in_specs=[hbm, hbm, vmem, vmem],
            out_specs=(vmem, vmem),
            scratch_shapes=[
                pltpu.VMEM((3 * SIDE, seg_rows, seg_rows), jnp.bfloat16),
                pltpu.VMEM((HALVES, 2, 2, SIDE) + panel, jnp.bfloat16),
                pltpu.VMEM((HALVES, DIAG_ACC + 1) + panel, jnp.float32),
                pltpu.VMEM((HALVES, SIDE + 1) + panel, jnp.float32),
                pltpu.VMEM((HALVES, 2, SIDE) + panel, jnp.float32),
                pltpu.VMEM((HALVES,) + panel, jnp.float32),
                pltpu.VMEM((HALVES,) + panel, jnp.float32),
                dma((3 * SIDE,)),
                dma((HALVES, 5, SIDE)),
                dma((HALVES, 2, SIDE)),
                dma((HALVES, 2, SIDE)),
                dma((HALVES, 2 * SIDE)),
                dma((HALVES, SIDE + 1)),
                dma((HALVES, 2, SIDE)),
            ],
            compiler_params=pltpu.CompilerParams(
                collective_id=0, has_side_effects=True, vmem_limit_bytes=67_000_000),
        )(h_slab[0, 0], h_diag[0], vec_occ.T, vec_virt.T)
        return filt_occ.T, filt_virt.T

    return jax.shard_map(local_filter, mesh=mesh, in_specs=(slab_spec, diag_spec, vec_spec, vec_spec), out_specs=(vec_spec, vec_spec), check_vma=False)
```

time: 703 us -> 212 us (0.30)
  the two profiles are of different devices: /device:TPU:0 before, /device:TPU:1 now
where the time goes in v1:
time: 212 us; the launch traced here: 211 us
  Pallas kernels  207 us (98%)
  local copies, waits for them, and re-layouts  3.44 us (2%)
    pallas_call x1, Pallas kernels, local_filter(): pl.pallas_call(filter_kernel, out_shape=(out, out), in_specs=[hbm, hbm, v...  207 us

profile of v1, /device:TPU:1, one launch (start us, length us, event | category | flops | bytes accessed | tf_op | source)
XLA Modules:
  0.0 211.3 jit_solution(12742150530318658670)
XLA Ops:
  0.6 207.2 %shard_map.59 = (f32[64,1280]{1,0:T(8,128)}, f32[64,1280]{1,0:T(8,128)}) custom-call(bf16[2560,5120]{1,0:T(8,128)(2,1)} %bitcast.6, bf16[1280,5120]{1,0:T(8,128)(2,1)} %bitcast.7, f32[64,1280]{1,0:T(8,128)} %bitcast.8, f32[64,1280]{1,0:T(8,128)} %bitcast.9), custom_call_target="tpu_custom_call" | custom-call | tf_op jit(solution)/shard_map/pallas_call | solution.py:430
  207.9 1.7 copy.8
  209.6 1.7 copy.9

commit v2 on v1

v2 whole, which is shorter than its diff:
```python
import jax
import jax.numpy as jnp
from jax import lax
from jax.experimental import pallas as pl
from jax.experimental.pallas import tpu as pltpu
from jax.sharding import PartitionSpec as P

FILTER_STEPS = 3
CEN_OCC = 0.5
CEN_VIRT = -0.5
HALF_WIDTH = 1.5
SIDE = 4
HALVES = 2
UNITS = FILTER_STEPS * HALVES
EARLY = 2
CHUNKS = 2
MESH = pl.DeviceIdType.MESH
NN = (((1,), (0,)), ((), ()))
NT = (((1,), (1,)), ((), ()))


def filter_kernel(slab_hbm, strip_hbm, occ_ref, virt_ref, out_occ, out_virt,
                  mat, vec, acc, strip_acc, red, col, cur, prev,
                  mat_sem, vec_send, vec_recv, colvec_recv, acc_send, red_recv, col_recv):
    seg_rows = cur.shape[-1]
    n_vecs = cur.shape[1]
    part = n_vecs // CHUNKS

    def rows_of(q):
        return pl.ds(q * part, part)

    def half_rows(h, q):
        return pl.ds(pl.multiple_of(h * n_vecs + q * part, part), part)

    def half_of(h):
        return pl.ds(pl.multiple_of(h * n_vecs, n_vecs), n_vecs)

    kpt = lax.axis_index("kpt")
    c = lax.axis_index("col")
    r = lax.axis_index("row")
    is_diag = r == c
    lower = r > c
    upper = r < c
    chip = r // 2
    core = r % 2
    partner = r + 1 - 2 * core
    same_chip = (c // 2) == chip
    far0 = 2 * (1 - chip)
    col_peers = (partner, far0, far0 + 1)
    diag_dev = (kpt, c, c)

    def seg_order(i):
        ahead = jnp.where(c == 1, jnp.where(i < 2, 3 - i, i - 2), jnp.where(i < 2, i, 5 - i))
        return jnp.where(c == 0, 3 - i, jnp.where(c == 3, i, ahead))

    def goes_right(cc, seg):
        return (seg < 2) | (r <= cc)

    def goes_left(cc, seg):
        return ~((r == 3) & (cc == 3) & (seg < 2))

    def sends(seg):
        return jnp.where(seg > c, goes_right(c, seg), goes_left(c, seg)) & (seg != c)

    def from_left(seg):
        return (c > 0) & goes_right(c - 1, seg)

    def from_right(seg):
        return (c < 3) & goes_left(c + 1, seg)

    def incoming(seg):
        return jnp.where(seg > c, from_left(seg), from_right(seg))

    def row_copy(h, b, seg, way, q):
        return pltpu.make_async_remote_copy(
            src_ref=vec.at[b, 0, seg, half_rows(h, q)], dst_ref=vec.at[b, 0, seg, half_rows(h, q)],
            send_sem=vec_send.at[h, way, seg, q], recv_sem=vec_recv.at[h, b, seg, q],
            device_id=(kpt, c + 1 - 2 * way, r), device_id_type=MESH)

    def col_copy(h, b, seg, peer, q):
        return pltpu.make_async_remote_copy(
            src_ref=vec.at[b, 0, seg, half_rows(h, q)], dst_ref=vec.at[b, 1, seg, half_rows(h, q)],
            send_sem=vec_send.at[h, 2 + peer, seg, q], recv_sem=colvec_recv.at[h, b, seg, q],
            device_id=(kpt, c, col_peers[peer]), device_id_type=MESH)

    def red_copy(h, seg, q):
        step = jnp.where(seg > c, 1, -1)
        slot = jnp.where(seg == c - 1, SIDE, seg)
        return pltpu.make_async_remote_copy(
            src_ref=acc.at[h, seg, rows_of(q)], dst_ref=red.at[h, slot, rows_of(q)],
            send_sem=acc_send.at[h, seg, q], recv_sem=red_recv.at[h, slot, q],
            device_id=(kpt, c + step, r), device_id_type=MESH)

    def sum_copy(h, seg, slot, dev, q):
        return pltpu.make_async_remote_copy(
            src_ref=acc.at[h, SIDE + seg, rows_of(q)], dst_ref=col.at[h, slot, seg, rows_of(q)],
            send_sem=acc_send.at[h, SIDE + seg, q], recv_sem=col_recv.at[h, slot, seg, q],
            device_id=dev, device_id_type=MESH)

    def send_row(h, b, seg, left_ok, right_ok, q):
        @pl.when((c < 3) & right_ok)
        def _():
            row_copy(h, b, seg, 0, q).start()

        @pl.when((c > 0) & left_ok)
        def _():
            row_copy(h, b, seg, 1, q).start()

    def send_col(h, b, seg, q):
        for peer in range(3):
            @pl.when(is_diag & ((col_peers[peer] > c) | (seg >= 2)))
            def _():
                col_copy(h, b, seg, peer, q).start()

    def wait_vec_sends(h, b):
        def each(seg, carry):
            for q in range(CHUNKS):
                @pl.when((c < 3) & (seg <= c))
                def _():
                    row_copy(h, b, seg, 0, q).wait_send()

                @pl.when((c > 0) & (seg >= c))
                def _():
                    row_copy(h, b, seg, 1, q).wait_send()

                for peer in range(3):
                    @pl.when(is_diag & ((col_peers[peer] > c) | (seg >= 2)))
                    def _():
                        col_copy(h, b, seg, peer, q).wait_send()
            return carry

        lax.fori_loop(0, SIDE, each, 0)

    def wait_acc_sends(h):
        def each(seg, carry):
            for q in range(CHUNKS):
                @pl.when(sends(seg))
                def _():
                    red_copy(h, seg, q).wait_send()

                @pl.when(~is_diag & (lower | (seg >= 2)))
                def _():
                    sum_copy(h, seg, 0, diag_dev, q).wait_send()
            return carry

        lax.fori_loop(0, SIDE, each, 0)

    def wait_colvec(h, b, seg):
        for q in range(CHUNKS):
            col_copy(h, b, seg, 0, q).wait_recv()

    def send_sum(h, seg):
        for q in range(CHUNKS):
            @pl.when(same_chip)
            def _():
                sum_copy(h, seg, 0, diag_dev, q).start()

            @pl.when(~same_chip & (seg % 2 != core))
            def _():
                sum_copy(h, seg, 0, (kpt, c, partner), q).start()

    def combine_sums(h):
        def each(i, carry):
            seg = 2 * (1 - i) + core
            for q in range(CHUNKS):
                sum_copy(h, seg, 0, diag_dev, q).wait_recv()
                acc[h, SIDE + seg, rows_of(q)] += col[h, 0, seg, rows_of(q)]
                sum_copy(h, seg, 1, diag_dev, q).start()
            return carry

        @pl.when(~same_chip)
        def _():
            lax.fori_loop(0, jnp.where(lower, 2, 1), each, 0)

    def column_total(h, start, stop):
        def each(i, carry):
            seg = seg_order(i)
            near = (partner > c) | (seg >= 2)
            far = (far0 > c) | (seg >= 2)
            for q in range(CHUNKS):
                @pl.when(near)
                def _():
                    sum_copy(h, seg, 0, diag_dev, q).wait_recv()
                    acc[h, seg, rows_of(q)] += col[h, 0, seg, rows_of(q)]

                @pl.when(far)
                def _():
                    sum_copy(h, seg, 1, diag_dev, q).wait_recv()
                    acc[h, seg, rows_of(q)] += col[h, 1, seg, rows_of(q)]
                start_sum(h, seg, q)
            return carry

        lax.fori_loop(start, stop, each, 0)

    def arrived(h, seg, slot, q):
        pltpu.make_async_remote_copy(
            src_ref=acc.at[h, seg, rows_of(q)], dst_ref=red.at[h, slot, rows_of(q)],
            send_sem=acc_send.at[h, seg, q], recv_sem=red_recv.at[h, slot, q],
            device_id=diag_dev, device_id_type=MESH).wait_recv()
        acc[h, seg, rows_of(q)] += red[h, slot, rows_of(q)]

    def relay(h, seg):
        @pl.when(sends(seg) & incoming(seg))
        def _():
            for q in range(CHUNKS):
                arrived(h, seg, seg, q)
                red_copy(h, seg, q).start()

    def start_sum(h, seg, q):
        @pl.when(sends(seg) & ~incoming(seg))
        def _():
            red_copy(h, seg, q).start()

    def product(left, right, dims):
        return lax.dot_general(left, right, dims, preferred_element_type=jnp.float32)

    first_half = jnp.where(c == 0, 0, 1)

    def slab_load(half, seg):
        rows = pl.ds(pl.multiple_of(half * seg_rows, seg_rows), seg_rows)
        return pltpu.make_async_copy(
            slab_hbm.at[rows, pl.ds(pl.multiple_of(seg * seg_rows, seg_rows), seg_rows)],
            mat.at[seg, rows], mat_sem.at[half, seg])

    def strip_load(seg):
        return pltpu.make_async_copy(
            strip_hbm.at[:, pl.ds(pl.multiple_of(seg * seg_rows, seg_rows), seg_rows)],
            mat.at[seg, pl.ds(2 * seg_rows, seg_rows)], mat_sem.at[2, seg])

    def strip_terms(k, b):
        strip_acc[...] = jnp.zeros_like(strip_acc)

        def each(seg, carry):
            @pl.when(k == 1)
            def _():
                strip_load(seg).wait()
            strip_acc[...] += product(vec[b, 0, seg], mat[seg, 2 * seg_rows:], NT)
            return carry

        lax.fori_loop(0, SIDE, each, 0)

    def take_piece(k, h, b, seg):
        @pl.when(upper)
        def _():
            @pl.when((k == 0) & ((c < 3) | (seg > 0)))
            def _():
                for half in range(2):
                    slab_load(half, seg).wait()
            both = product(vec[b, 0, seg, half_of(h)], mat[seg, :2 * seg_rows], NT)
            for i in range(2):
                acc[h, SIDE + 2 + i] += both[:, i * seg_rows:(i + 1) * seg_rows]

        @pl.when(lower & (seg < 2))
        def _():
            @pl.when(k == 0)
            def _():
                for j in range(SIDE):
                    slab_load(seg, j).wait()

                @pl.when(seg == first_half)
                def _():
                    for j in range(SIDE):
                        slab_load(1 - first_half, j).start()
            rows = pl.ds(pl.multiple_of(seg * seg_rows, seg_rows), seg_rows)
            for j in range(SIDE):
                acc[h, SIDE + j] += product(vec[b, 0, seg, half_of(h)], mat[j, rows], NN)

    def upper_row_terms(h, b):
        def each(i, carry):
            seg = seg_order(i)
            acc[h, seg] = (product(vec[b, 1, 2, half_of(h)], mat[seg, :seg_rows], NN)
                           + product(vec[b, 1, 3, half_of(h)], mat[seg, seg_rows:2 * seg_rows], NN))

            @pl.when(i < EARLY)
            def _():
                for q in range(CHUNKS):
                    start_sum(h, seg, q)
            return carry

        lax.fori_loop(0, SIDE, each, 0)

    def lower_row_terms(h, b):
        def each(i, carry):
            seg = (i + c) % SIDE

            @pl.when(i > 0)
            def _():
                wait_colvec(h, b, seg)
            both = product(vec[b, 1, seg, half_of(h)], mat[seg, :2 * seg_rows], NT)
            for half in range(2):
                acc[h, half] += both[:, half * seg_rows:(half + 1) * seg_rows]
            return carry

        lax.fori_loop(0, SIDE, each, 0)

    def finish(k, h, b, next_b):
        wait_vec_sends(h, b)

        for q in range(CHUNKS):
            @pl.when(from_left(c))
            def _():
                arrived(h, c, c, q)

            @pl.when(from_right(c))
            def _():
                arrived(h, c, SIDE, q)

        center = jnp.where(h == 0, CEN_OCC, CEN_VIRT)
        applied = acc[h, c] + strip_acc[half_of(h)]
        scaled = (applied - center * cur[h]) * (1.0 / HALF_WIDTH)
        first = k < HALVES
        nxt = jnp.where(first, scaled, 2.0 * scaled - prev[h])
        prev[h] = cur[h]
        cur[h] = nxt

        @pl.when(k + HALVES < UNITS)
        def _():
            vec[next_b, 0, c, half_of(h)] = nxt.astype(jnp.bfloat16)
            for q in range(CHUNKS):
                send_row(h, next_b, c, True, True, q)
                send_col(h, next_b, c, q)

    barrier = pltpu.get_barrier_semaphore()

    @pl.when(c > 0)
    def _():
        pl.semaphore_signal(barrier, inc=1, device_id=(kpt, c - 1, r), device_id_type=MESH)

    @pl.when(c < 3)
    def _():
        pl.semaphore_signal(barrier, inc=1, device_id=(kpt, c + 1, r), device_id_type=MESH)

    for peer in range(3):
        pl.semaphore_signal(barrier, inc=1, device_id=(kpt, c, col_peers[peer]), device_id_type=MESH)

    def load_block(i, carry):
        seg = (c + i) % SIDE

        @pl.when(upper)
        def _():
            for half in range(2):
                slab_load(half, seg).start()

        @pl.when(lower)
        def _():
            slab_load(first_half, seg).start()
        return carry

    lax.fori_loop(0, SIDE, load_block, 0)
    for h, src in enumerate((occ_ref, virt_ref)):
        cur[h] = src[...]
        prev[h] = jnp.zeros_like(src)
        vec[0, 0, c, half_of(h)] = src[...].astype(jnp.bfloat16)
    pl.semaphore_wait(barrier, 3 + (c > 0).astype(jnp.int32) + (c < 3).astype(jnp.int32))
    for q in range(CHUNKS):
        send_row(0, 0, c, True, True, q)
        send_col(0, 0, c, q)

    def slot(k, carry):
        h = k % 2
        b = (k // 2) % 2
        last = k - 1
        lh = (k + 1) % 2
        lb = ((k + 1) // 2 + 1) % 2
        live = k < UNITS
        older = k >= 1

        @pl.when(live)
        def _():
            @pl.when(k >= HALVES)
            def _():
                wait_acc_sends(h)

            def clear(i, cc):
                acc[h, i] = jnp.zeros(acc.shape[2:], acc.dtype)
                return cc

            lax.fori_loop(0, 2 * SIDE, clear, 0)

        def arrivals(d, cc):
            for q in range(CHUNKS):
                for s in range(2):
                    seg = c + (2 * s - 1) * d

                    @pl.when(live & (seg >= 0) & (seg < SIDE) & (d > 0))
                    def _():
                        row_copy(h, b, seg, 0, q).wait_recv()
                        send_row(h, b, seg, s == 1, s == 0, q)
                        send_col(h, b, seg, q)

            @pl.when(older & is_diag & (c >= 2) & (d == 1))
            def _():
                column_total(lh, 0, SIDE)

            def hop(i):
                @pl.when(older & (c > 0) & (c < 3) & (i >= 0) & (i < 3))
                def _():
                    relay(lh, jnp.where(c == 1, jnp.where(i == 2, 0, 3 - i), jnp.where(i == 2, 3, i)))

            hop(d - 1 - 5 * (d == 3))

            @pl.when((k == 0) & (d == 2))
            def _():
                for q in range(CHUNKS):
                    send_row(1, 0, c, True, True, q)
                    send_col(1, 0, c, q)

            def use(s, ccc):
                seg = c + (2 * s - 1) * d

                @pl.when(live & (seg >= 0) & (seg < SIDE) & ((d > 0) | (s == 0)))
                def _():
                    take_piece(k, h, b, seg)
                return ccc

            lax.fori_loop(0, 2, use, 0)

            hop(jnp.where(d == 2, 2, -1))

            @pl.when(live & lower & (d == jnp.where(c == 2, 2, 1)))
            def _():
                wait_colvec(h, b, c)

                def each(i, ccc):
                    send_sum(h, seg_order(i))
                    return ccc

                lax.fori_loop(0, SIDE, each, 0)

            @pl.when(live & lower & (d == 2))
            def _():
                combine_sums(h)

            @pl.when(live & upper & (d == 2))
            def _():
                wait_colvec(h, b, 2)
                wait_colvec(h, b, 3)

                @pl.when((k == 0) & (c == 3))
                def _():
                    for half in range(2):
                        slab_load(half, 0).wait()
                upper_row_terms(h, b)
            return cc

        lax.fori_loop(0, SIDE, arrivals, 0)

        @pl.when(k == 0)
        def _():
            for j in range(SIDE):
                strip_load(j).start()

        @pl.when(live & upper)
        def _():
            send_sum(h, 2)
            send_sum(h, 3)

        @pl.when(live & lower)
        def _():
            lower_row_terms(h, b)

        @pl.when(live & is_diag & (c < 2))
        def _():
            column_total(h, 0, 2)

        @pl.when(live & (h == 1))
        def _():
            strip_terms(k, b)

        @pl.when(older)
        def _():
            finish(last, lh, lb, 1 - lb)

        @pl.when(live & ~is_diag)
        def _():
            def each(i, cc):
                for q in range(CHUNKS):
                    start_sum(h, seg_order(i), q)
                return cc

            lax.fori_loop(jnp.where(upper, EARLY, 0), SIDE, each, 0)

        @pl.when(live & upper)
        def _():
            combine_sums(h)

        @pl.when(live & is_diag & (c < 2))
        def _():
            column_total(h, 2, SIDE)
        return carry

    lax.fori_loop(0, UNITS + 1, slot, 0)
    for h in range(HALVES):
        wait_acc_sends(h)
    out_occ[...] = cur[0]
    out_virt[...] = cur[1]


def solution(mesh):
    slab_spec = P(("kpt", "row"), "col", None, None)
    diag_spec = P(("kpt", "row"), "col", None)
    vec_spec = P(("kpt", "row", "col"), None)

    def local_filter(h_slab, h_diag, vec_occ, vec_virt):
        seg_rows, n_vecs = vec_occ.shape
        panel = (n_vecs, seg_rows)
        out = jax.ShapeDtypeStruct(panel, jnp.float32)
        vmem = pl.BlockSpec(memory_space=pltpu.VMEM)
        hbm = pl.BlockSpec(memory_space=pl.ANY)
        dma = pltpu.SemaphoreType.DMA
        filt_occ, filt_virt = pl.pallas_call(
            filter_kernel,
            out_shape=(out, out),
            in_specs=[hbm, hbm, vmem, vmem],
            out_specs=(vmem, vmem),
            scratch_shapes=[
                pltpu.VMEM((SIDE, 3 * seg_rows, seg_rows), jnp.bfloat16),
                pltpu.VMEM((2, 2, SIDE, HALVES * n_vecs, seg_rows), jnp.bfloat16),
                pltpu.VMEM((HALVES, 2 * SIDE) + panel, jnp.float32),
                pltpu.VMEM((HALVES * n_vecs, seg_rows), jnp.float32),
                pltpu.VMEM((HALVES, SIDE + 1) + panel, jnp.float32),
                pltpu.VMEM((HALVES, 2, SIDE) + panel, jnp.float32),
                pltpu.VMEM((HALVES,) + panel, jnp.float32),
                pltpu.VMEM((HALVES,) + panel, jnp.float32),
                dma((3, SIDE)),
                dma((HALVES, 5, SIDE, CHUNKS)),
                dma((HALVES, 2, SIDE, CHUNKS)),
                dma((HALVES, 2, SIDE, CHUNKS)),
                dma((HALVES, 2 * SIDE, CHUNKS)),
                dma((HALVES, SIDE + 1, CHUNKS)),
                dma((HALVES, 2, SIDE, CHUNKS)),
            ],
            compiler_params=pltpu.CompilerParams(
                collective_id=0, has_side_effects=True, vmem_limit_bytes=67_000_000),
        )(h_slab[0, 0], h_diag[0], vec_occ.T, vec_virt.T)
        return filt_occ.T, filt_virt.T

    return jax.shard_map(local_filter, mesh=mesh, in_specs=(slab_spec, diag_spec, vec_spec, vec_spec), out_specs=(vec_spec, vec_spec), check_vma=False)
```

time: 212 us -> 185 us (0.87)
  the two profiles are of different devices: /device:TPU:1 before, /device:TPU:6 now
where the time goes in v2:
time: 185 us
  Pallas kernels  181 us (98%)
  local copies, waits for them, and re-layouts  3.44 us (2%)
    pallas_call x1, Pallas kernels, local_filter(): pl.pallas_call(filter_kernel, out_shape=(out, out), in_specs=[hbm, hbm, v...  181 us

profile of v2, /device:TPU:6, one launch (start us, length us, event | category | flops | bytes accessed | tf_op | source)
XLA Modules:
  0.0 185.1 jit_solution(1473481424490604051)
XLA Ops:
  0.6 181.0 %shard_map.59 = (f32[64,1280]{1,0:T(8,128)}, f32[64,1280]{1,0:T(8,128)}) custom-call(bf16[2560,5120]{1,0:T(8,128)(2,1)} %bitcast.6, bf16[1280,5120]{1,0:T(8,128)(2,1)} %bitcast.7, f32[64,1280]{1,0:T(8,128)} %bitcast.8, f32[64,1280]{1,0:T(8,128)} %bitcast.9), custom_call_target="tpu_custom_call" | custom-call | tf_op jit(solution)/shard_map/pallas_call | solution.py:511
  181.7 1.7 copy.8
  183.4 1.7 copy.9

commit v3 on v2

--- a/solution.py
+++ b/solution.py
@@ -19,7 +19,7 @@
 NT = (((1,), (1,)), ((), ()))
 
 
-def filter_kernel(slab_hbm, strip_hbm, occ_ref, virt_ref, out_occ, out_virt,
+def filter_kernel(slab_hbm, strip_hbm, occ_ref, virt_ref, out,
                   mat, vec, acc, strip_acc, red, col, cur, prev,
                   mat_sem, vec_send, vec_recv, colvec_recv, acc_send, red_recv, col_recv):
     seg_rows = cur.shape[-1]
@@ -227,17 +227,12 @@
             strip_hbm.at[:, pl.ds(pl.multiple_of(seg * seg_rows, seg_rows), seg_rows)],
             mat.at[seg, pl.ds(2 * seg_rows, seg_rows)], mat_sem.at[2, seg])
 
-    def strip_terms(k, b):
-        strip_acc[...] = jnp.zeros_like(strip_acc)
-
-        def each(seg, carry):
-            @pl.when(k == 1)
-            def _():
-                strip_load(seg).wait()
-            strip_acc[...] += product(vec[b, 0, seg], mat[seg, 2 * seg_rows:], NT)
-            return carry
-
-        lax.fori_loop(0, SIDE, each, 0)
+    def strip_terms(k, b, seg, first):
+        @pl.when(k == 1)
+        def _():
+            strip_load(seg).wait()
+        term = product(vec[b, 0, seg], mat[seg, 2 * seg_rows:], NT)
+        strip_acc[...] = jnp.where(first, 0.0, strip_acc[...]) + term
 
     def take_piece(k, h, b, seg):
         @pl.when(upper)
@@ -378,8 +373,8 @@
             lax.fori_loop(0, 2 * SIDE, clear, 0)
 
         def arrivals(d, cc):
-            for q in range(CHUNKS):
-                for s in range(2):
+            for s in (1, 0):
+                for q in range(CHUNKS):
                     seg = c + (2 * s - 1) * d
 
                     @pl.when(live & (seg >= 0) & (seg < SIDE) & (d > 0))
@@ -411,6 +406,10 @@
                 @pl.when(live & (seg >= 0) & (seg < SIDE) & ((d > 0) | (s == 0)))
                 def _():
                     take_piece(k, h, b, seg)
+
+                    @pl.when(h == 1)
+                    def _():
+                        strip_terms(k, b, seg, d == 0)
                 return ccc
 
             lax.fori_loop(0, 2, use, 0)
@@ -459,13 +458,9 @@
         def _():
             lower_row_terms(h, b)
 
-        @pl.when(live & is_diag & (c < 2))
+        @pl.when(live & is_diag & (c == 0))
         def _():
             column_total(h, 0, 2)
-
-        @pl.when(live & (h == 1))
-        def _():
-            strip_terms(k, b)
 
         @pl.when(older)
         def _():
@@ -486,14 +481,14 @@
 
         @pl.when(live & is_diag & (c < 2))
         def _():
-            column_total(h, 2, SIDE)
+            column_total(h, jnp.where(c == 0, 2, 0), SIDE)
         return carry
 
     lax.fori_loop(0, UNITS + 1, slot, 0)
     for h in range(HALVES):
         wait_acc_sends(h)
-    out_occ[...] = cur[0]
-    out_virt[...] = cur[1]
+    for h in range(HALVES):
+        out[h * n_vecs:(h + 1) * n_vecs] = cur[h]
 
 
 def solution(mesh):
@@ -504,15 +499,14 @@
     def local_filter(h_slab, h_diag, vec_occ, vec_virt):
         seg_rows, n_vecs = vec_occ.shape
         panel = (n_vecs, seg_rows)
-        out = jax.ShapeDtypeStruct(panel, jnp.float32)
         vmem = pl.BlockSpec(memory_space=pltpu.VMEM)
         hbm = pl.BlockSpec(memory_space=pl.ANY)
         dma = pltpu.SemaphoreType.DMA
-        filt_occ, filt_virt = pl.pallas_call(
+        both = pl.pallas_call(
             filter_kernel,
-            out_shape=(out, out),
+            out_shape=jax.ShapeDtypeStruct((HALVES * n_vecs, seg_rows), jnp.float32),
             in_specs=[hbm, hbm, vmem, vmem],
-            out_specs=(vmem, vmem),
+            out_specs=vmem,
             scratch_shapes=[
                 pltpu.VMEM((SIDE, 3 * seg_rows, seg_rows), jnp.bfloat16),
                 pltpu.VMEM((2, 2, SIDE, HALVES * n_vecs, seg_rows), jnp.bfloat16),
@@ -533,6 +527,6 @@
             compiler_params=pltpu.CompilerParams(
                 collective_id=0, has_side_effects=True, vmem_limit_bytes=67_000_000),
         )(h_slab[0, 0], h_diag[0], vec_occ.T, vec_virt.T)
-        return filt_occ.T, filt_virt.T
+        return both[:n_vecs].T, both[n_vecs:].T
 
     return jax.shard_map(local_filter, mesh=mesh, in_specs=(slab_spec, diag_spec, vec_spec, vec_spec), out_specs=(vec_spec, vec_spec), check_vma=False)

time: 185 us -> 179 us (0.968)
  the two profiles are of different devices: /device:TPU:6 before, /device:TPU:0 now
where the time goes in v3:
time: 179 us
  Pallas kernels  176 us (98%)
  local copies, waits for them, and re-layouts  1.95 us (1%)
    pallas_call x1, Pallas kernels, local_filter(): pl.pallas_call(filter_kernel, out_shape=jax.ShapeDtypeStruct((HALVES * n_...  176 us

profile of v3, /device:TPU:0, one launch (start us, length us, event | category | flops | bytes accessed | tf_op | source)
XLA Modules:
  0.0 178.8 jit_solution(1064213739627690453)
XLA Ops:
  0.6 176.2 %shard_map.59 = f32[128,1280]{1,0:T(8,128)} custom-call(bf16[2560,5120]{1,0:T(8,128)(2,1)} %bitcast.8, bf16[1280,5120]{1,0:T(8,128)(2,1)} %bitcast.9, f32[64,1280]{1,0:T(8,128)} %bitcast.10, f32[64,1280]{1,0:T(8,128)} %bitcast.11), custom_call_target="tpu_custom_call" | custom-call | tf_op jit(solution)/shard_map/pallas_call | solution.py:505
  176.9 1.9 %slice_bitcast_fusion = (f32[1280,64]{0,1:T(8,128)}, f32[1280,64]{0,1:T(8,128)}) fusion(f32[128,1280]{1,0:T(8,128)} %shard_map.59), kind=kLoop, calls=%fused_computation | loop fusion | bytes 1310720 | tf_op jit(solution)/shard_map/transpose | solution.py:530

commit v4 on v3

--- a/solution.py
+++ b/solution.py
@@ -260,13 +260,13 @@
             for j in range(SIDE):
                 acc[h, SIDE + j] += product(vec[b, 0, seg, half_of(h)], mat[j, rows], NN)
 
-    def upper_row_terms(h, b):
+    def upper_row_terms(h, b, early):
         def each(i, carry):
             seg = seg_order(i)
             acc[h, seg] = (product(vec[b, 1, 2, half_of(h)], mat[seg, :seg_rows], NN)
                            + product(vec[b, 1, 3, half_of(h)], mat[seg, seg_rows:2 * seg_rows], NN))
 
-            @pl.when(i < EARLY)
+            @pl.when(i < early)
             def _():
                 for q in range(CHUNKS):
                     start_sum(h, seg, q)
@@ -359,6 +359,8 @@
         lb = ((k + 1) // 2 + 1) % 2
         live = k < UNITS
         older = k >= 1
+        final = k == UNITS - 1
+        early = jnp.where(final, SIDE, EARLY)
 
         @pl.when(live)
         def _():
@@ -439,7 +441,7 @@
                 def _():
                     for half in range(2):
                         slab_load(half, 0).wait()
-                upper_row_terms(h, b)
+                upper_row_terms(h, b, early)
             return cc
 
         lax.fori_loop(0, SIDE, arrivals, 0)
@@ -462,26 +464,35 @@
         def _():
             column_total(h, 0, 2)
 
+        def send_terms():
+            @pl.when(live & ~is_diag)
+            def _():
+                def each(i, cc):
+                    for q in range(CHUNKS):
+                        start_sum(h, seg_order(i), q)
+                    return cc
+
+                lax.fori_loop(jnp.where(upper, early, 0), SIDE, each, 0)
+
+            @pl.when(live & upper)
+            def _():
+                combine_sums(h)
+
+            @pl.when(live & is_diag & (c < 2))
+            def _():
+                column_total(h, jnp.where(c == 0, 2, 0), SIDE)
+
+        @pl.when(final)
+        def _():
+            send_terms()
+
         @pl.when(older)
         def _():
             finish(last, lh, lb, 1 - lb)
 
-        @pl.when(live & ~is_diag)
-        def _():
-            def each(i, cc):
-                for q in range(CHUNKS):
-                    start_sum(h, seg_order(i), q)
-                return cc
-
-            lax.fori_loop(jnp.where(upper, EARLY, 0), SIDE, each, 0)
-
-        @pl.when(live & upper)
-        def _():
-            combine_sums(h)
-
-        @pl.when(live & is_diag & (c < 2))
-        def _():
-            column_total(h, jnp.where(c == 0, 2, 0), SIDE)
+        @pl.when(~final)
+        def _():
+            send_terms()
         return carry
 
     lax.fori_loop(0, UNITS + 1, slot, 0)

time: 179 us -> 179 us (level)
  no operation moved by 1% of the time
where the time goes in v4:
time: 179 us
  Pallas kernels  176 us (98%)
  local copies, waits for them, and re-layouts  1.95 us (1%)
    pallas_call x1, Pallas kernels, local_filter(): pl.pallas_call(filter_kernel, out_shape=jax.ShapeDtypeStruct((HALVES * n_...  176 us

profile of v4, /device:TPU:0, one launch (start us, length us, event | category | flops | bytes accessed | tf_op | source)
XLA Modules:
  0.0 178.8 jit_solution(10963744683553617881)
XLA Ops:
  0.6 176.2 %shard_map.59 = f32[128,1280]{1,0:T(8,128)} custom-call(bf16[2560,5120]{1,0:T(8,128)(2,1)} %bitcast.8, bf16[1280,5120]{1,0:T(8,128)(2,1)} %bitcast.9, f32[64,1280]{1,0:T(8,128)} %bitcast.10, f32[64,1280]{1,0:T(8,128)} %bitcast.11), custom_call_target="tpu_custom_call" | custom-call | tf_op jit(solution)/shard_map/pallas_call | solution.py:516
  176.8 1.9 %slice_bitcast_fusion = (f32[1280,64]{0,1:T(8,128)}, f32[1280,64]{0,1:T(8,128)}) fusion(f32[128,1280]{1,0:T(8,128)} %shard_map.59), kind=kLoop, calls=%fused_computation | loop fusion | bytes 1310720 | tf_op jit(solution)/shard_map/transpose | solution.py:541
